TPU v7x, 32 devices: a whole 2x2x4 slice. The times are simulated.
32 devices in a mesh: tm: 16 (over z, x, core), space: 2 (over y).
Axes of the slice: x: 2, y: 2, z: 4, core: 2. Of those that a mesh axis runs over, the one named last changes fastest.
Arguments:
- fine_nodes: float32 [16, 3, 3, 32, 4096], P('tm', None, None, 'space'), may hold values from -6 to 6
- init_state: float32 [3, 32, 4096], P(None, 'space'), may hold values from -6 to 6
- mean_depth: float32 [32, 4096], P('space'), may hold values from 0.5 to 2
Outputs:
- new_nodes: float32 [16, 3, 3, 32, 4096], P('tm', None, None, 'space')
All inputs are finite; a program needn't handle non-finite values.
Results may differ from a plain program's by a relative error of at most 0.00002.
Values sent between devices are 32-bit elements; how exact they have to be, the bound alone decides.
A program may use at most 64 MiB of HBM per device.

v0:
```python
import jax
import jax.numpy as jnp
from jax import lax
from jax.sharding import PartitionSpec as P

step_size = 0.3
viscosity = 1.0 / 3.0
coriolis = 0.5
quad_near = 5.0 / 24.0
quad_mid = 1.0 / 3.0
quad_far = -1.0 / 24.0


def from_behind(value, axis, by):
    peers = lax.axis_size(axis)
    pairs = [(i, i + by) for i in range(peers) if 0 <= i + by < peers]
    return lax.ppermute(value, axis, pairs)


def extended(cells, sides, width):
    for axis, dim in sides:
        count = lax.axis_size(axis)
        head = lax.slice_in_dim(cells, 0, width, axis=dim)
        tail = lax.slice_in_dim(cells, cells.shape[dim] - width, cells.shape[dim], axis=dim)
        cells = jnp.concatenate(
            [
                lax.ppermute(tail, axis, [(i, (i + 1) % count) for i in range(count)]),
                cells,
                lax.ppermute(head, axis, [((i + 1) % count, i) for i in range(count)]),
            ],
            axis=dim,
        )
    return cells


def column_slope(values):
    return (jnp.roll(values, -1, -1) - jnp.roll(values, 1, -1)) * 0.5


def row_slope(values):
    return (values[..., 2:, :] - values[..., :-2, :]) * 0.5


def diffuse(values, centre):
    return (
        values[..., 2:, :]
        + values[..., :-2, :]
        + jnp.roll(centre, -1, -1)
        + jnp.roll(centre, 1, -1)
        - 4.0 * centre
    )


def tendency(padded, depth_rows):
    height = padded[..., 0, :, :]
    east_flow = padded[..., 1, :, :]
    north_flow = padded[..., 2, :, :]
    centre = padded[..., 1:-1, :]
    height_c = centre[..., 0, :, :]
    east_c = centre[..., 1, :, :]
    north_c = centre[..., 2, :, :]
    depth_c = depth_rows[1:-1]
    height_rate = (
        -column_slope(depth_c * east_c)
        - row_slope(depth_rows * north_flow)
        + viscosity * diffuse(height, height_c)
    )
    east_rate = (
        -column_slope(height_c) + coriolis * north_c + viscosity * diffuse(east_flow, east_c)
    )
    north_rate = -row_slope(height) - coriolis * east_c + viscosity * diffuse(north_flow, north_c)
    return jnp.stack([height_rate, east_rate, north_rate], axis=-3)


def per_device(fine_nodes, init_state, mean_depth):
    points = fine_nodes[0]
    row_count = points.shape[-2]
    col_count = points.shape[-1]
    half_step = step_size * 0.5
    is_first = lax.axis_index("tm") == 0
    previous = from_behind(points[2], "tm", 1)
    section_zero = jnp.where(is_first, init_state, previous)
    stacked = jnp.concatenate([points.reshape(9, row_count, col_count), mean_depth[None]], axis=0)
    widened_old = extended(stacked, (("space", 1),), 1)
    depth_rows = widened_old[9]
    old_rates = tendency(widened_old[:9].reshape(3, 3, row_count + 2, col_count), depth_rows)

    def fresh_rate(values):
        return tendency(extended(values, (("space", 1),), 1), depth_rows)

    rate_zero = fresh_rate(section_zero)
    section_one = (
        section_zero
        + half_step * (rate_zero - old_rates[0])
        + step_size * (quad_near * old_rates[0] + quad_mid * old_rates[1] + quad_far * old_rates[2])
    )
    rate_one = fresh_rate(section_one)
    section_two = (
        section_one
        + half_step * (rate_one - old_rates[1])
        + step_size * (quad_far * old_rates[0] + quad_mid * old_rates[1] + quad_near * old_rates[2])
    )
    rate_two = fresh_rate(section_two)
    fas_term = -(step_size / 3.0) * (rate_zero - 2.0 * rate_one + rate_two)
    drift_total = half_step * (rate_two - rate_zero) + fas_term
    boosted = drift_total + jnp.where(is_first, section_zero + step_size * rate_zero, 0.0)
    coarse_end = boosted
    offset = 1
    while offset < lax.axis_size("tm"):

        def one_layer(turn_index, values):
            padded = extended(values, (("space", 1),), 1)
            return values + step_size * tendency(padded, depth_rows)

        powered = lax.fori_loop(0, offset, one_layer, coarse_end)
        coarse_end = coarse_end + from_behind(powered, "tm", offset)
        offset = offset * 2
    previous_end = from_behind(coarse_end, "tm", 1)
    coarse_begin = jnp.where(is_first, init_state, previous_end)
    middle = section_one + 0.5 * (coarse_begin - section_zero + (coarse_end - section_two))
    return jnp.stack([coarse_begin, middle, coarse_end], axis=0)[None]


def solution(mesh):
    placed = (P("tm", None, None, "space", None), P(None, "space", None), P("space", None))
    return jax.shard_map(
        per_device,
        mesh=mesh,
        in_specs=placed,
        out_specs=P("tm", None, None, "space", None),
        check_vma=False,
    )
```

profile of v0, /device:TPU:26, one launch (start us, length us, event | category | flops | bytes accessed | tf_op | source)
XLA Modules:
  0.0 359.5 jit_solution(11264127611526048754)
XLA Ops:
  0.0 2.0 pad_maximum_fusion.46
  4.1 2.1 slice_bitcast_fusion.53
  6.2 1.9 collective-permute-start.6
  9.2 2.4 collective-permute-done.7
  11.6 2.3 pad_maximum_fusion.12
  17.2 2.5 collective-permute-done.6
  22.6 1.9 collective-permute-done.10
  32.6 1.9 collective-permute-done.11
  39.9 2.0 collective-permute-done.13
  47.6 1.9 collective-permute-done.15
  52.8 1.9 collective-permute-start.17
  54.7 11.7 %collective-permute-done.17 = f32[3,16,4096]{2,1,0:T(8,128)} collective-permute-done((f32[3,16,4096]{2,1,0:T(8,128)}, f32[3,16,4096]{2,1,0:T(8,128)}, u32[]{:S(2)}, u32[]{:S(2)}) %collective-permute-start.17) | collective-permute-done | bytes 786464 | tf_op jit(solution)/shard_map/ppermute | solution.py:17
  66.4 2.0 fusion.250
  69.4 29.0 %while.34 = (s32[]{:T(128)}, f32[3,16,4096]{2,1,0:T(8,128)S(1)}, f32[18,4096]{1,0:T(8,128)S(1)}, s32[]{:T(128)}, s32[]{}, /*index=5*/s32[]{}) while((s32[]{:T(128)}, f32[3,16,4096]{2,1,0:T(8,128)S(1)}, f32[18,4096]{1,0:T(8,128)S(1)}, s32[]{:T(128)}, s32[]{}, /*index=5*/s32[]{}) %tuple.247), condition=%wide.region_1.2_spmd, body=%wide.region_0.1_spmd.sunk | while | flops 4415490 | bytes 29294428 | solution.py:115
  76.7 1.8 dynamic-update-slice.16
  91.2 1.8 dynamic-update-slice.16
  99.7 17.0 %collective-permute-done.18 = f32[3,16,4096]{2,1,0:T(8,128)} collective-permute-done((f32[3,16,4096]{2,1,0:T(8,128)S(1)}, f32[3,16,4096]{2,1,0:T(8,128)}, u32[]{:S(2)}, u32[]{:S(2)}) %collective-permute-start.18) | collective-permute-done | bytes 786464 | tf_op jit(solution)/shard_map/ppermute | solution.py:17
  119.1 58.1 %while.35 = (s32[]{:T(128)}, f32[3,16,4096]{2,1,0:T(8,128)S(1)}, f32[18,4096]{1,0:T(8,128)S(1)}, s32[]{:T(128)}, s32[]{}, /*index=5*/s32[]{}) while((s32[]{:T(128)}, f32[3,16,4096]{2,1,0:T(8,128)S(1)}, f32[18,4096]{1,0:T(8,128)S(1)}, s32[]{:T(128)}, s32[]{}, /*index=5*/s32[]{}) %tuple.256), condition=%wide.region_3.4_spmd, body=%wide.region_2.3_spmd.sunk | while | flops 4415490 | bytes 29294428 | solution.py:115
  126.4 1.8 dynamic-update-slice.18
  140.9 1.8 dynamic-update-slice.18
  155.4 1.8 dynamic-update-slice.18
  169.9 1.8 dynamic-update-slice.18
  178.4 16.6 %collective-permute-done.19 = f32[3,16,4096]{2,1,0:T(8,128)S(1)} collective-permute-done((f32[3,16,4096]{2,1,0:T(8,128)S(1)}, f32[3,16,4096]{2,1,0:T(8,128)S(1)}, u32[]{:S(2)}, u32[]{:S(2)}) %collective-permute-start.19) | collective-permute-done | bytes 786464 | tf_op jit(solution)/shard_map/ppermute | solution.py:17
  197.2 116.1 %while.36 = (s32[]{:T(128)}, f32[3,16,4096]{2,1,0:T(8,128)S(1)}, f32[18,4096]{1,0:T(8,128)S(1)}, s32[]{:T(128)}, s32[]{}, /*index=5*/s32[]{}) while((s32[]{:T(128)}, f32[3,16,4096]{2,1,0:T(8,128)S(1)}, f32[18,4096]{1,0:T(8,128)S(1)}, s32[]{:T(128)}, s32[]{}, /*index=5*/s32[]{}) %tuple.257), condition=%wide.region_5.6_spmd, body=%wide.region_4.5_spmd.sunk | while | flops 4415490 | bytes 29294428 | solution.py:115
  204.5 1.8 dynamic-update-slice.20
  219.1 1.8 dynamic-update-slice.20
  248.1 1.8 dynamic-update-slice.20
  262.6 1.8 dynamic-update-slice.20
  277.1 1.8 dynamic-update-slice.20
  314.8 28.3 %collective-permute-done.20 = f32[3,16,4096]{2,1,0:T(8,128)S(1)} collective-permute-done((f32[3,16,4096]{2,1,0:T(8,128)S(1)}, f32[3,16,4096]{2,1,0:T(8,128)S(1)}, u32[]{:S(2)}, u32[]{:S(2)}) %collective-permute-start.20) | collective-permute-done | bytes 786464 | tf_op jit(solution)/shard_map/ppermute | solution.py:17
  344.3 1.9 collective-permute-start.21
  346.2 11.4 %collective-permute-done.21 = f32[3,16,4096]{2,1,0:T(8,128)S(1)} collective-permute-done((f32[3,16,4096]{2,1,0:T(8,128)S(1)}, f32[3,16,4096]{2,1,0:T(8,128)S(1)}, u32[]{:S(2)}, u32[]{:S(2)}) %collective-permute-start.21) | collective-permute-done | bytes 786464 | tf_op jit(solution)/shard_map/ppermute | solution.py:17
  (599 shorter events, 225.7 us)
Async XLA Ops:
  2.1 7.1 %collective-permute-start.8 = (f32[10,1,4096]{2,1,0:T(1,128)S(1)}, f32[10,1,4096]{2,1,0:T(1,128)S(1)}, u32[]{:S(2)}, u32[]{:S(2)}) collective-permute-start(f32[10,1,4096]{2,1,0:T(1,128)S(1)} %get-tuple-element.205), channel_id=1, source_target_pairs={{1,0},{0,1},{3,2},{2,3},{5,4},{4,5},{7,6},{6,7},{9,8},{8,9},{11,10... | collective-permute-start | bytes 491528 | tf_op jit(solution)/shard_map/ppermute | solution.py:29
  3.6 7.9 %collective-permute-start.7 = (f32[10,1,4096]{2,1,0:T(1,128)S(1)}, f32[10,1,4096]{2,1,0:T(1,128)S(1)}, u32[]{:S(2)}, u32[]{:S(2)}) collective-permute-start(f32[10,1,4096]{2,1,0:T(1,128)S(1)} %get-tuple-element.204), channel_id=1, source_target_pairs={{0,1},{1,0},{2,3},{3,2},{4,5},{5,4},{6,7},{7,6},{8,9},{9,8},{10,11... | collective-permute-start | bytes 491528 | tf_op jit(solution)/shard_map/ppermute | solution.py:27
  6.2 13.5 %collective-permute-start.6 = (f32[3,16,4096]{2,1,0:T(8,128)}, f32[3,16,4096]{2,1,0:T(8,128)S(1)}, u32[]{:S(2)}, u32[]{:S(2)}) collective-permute-start(f32[3,16,4096]{2,1,0:T(8,128)} %slice_bitcast_fusion.53), channel_id=1, source_target_pairs={{0,2},{2,4},{4,6},{6,8},{8,10},{10,12},{12,14},{14,16},{16,18},{18... | collective-permute-start | bytes 2359304 | tf_op jit(solution)/shard_map/ppermute | solution.py:17
  52.8 13.6 %collective-permute-start.17 = (f32[3,16,4096]{2,1,0:T(8,128)}, f32[3,16,4096]{2,1,0:T(8,128)}, u32[]{:S(2)}, u32[]{:S(2)}) collective-permute-start(f32[3,16,4096]{2,1,0:T(8,128)} %fusion.96), channel_id=1, source_target_pairs={{0,2},{2,4},{4,6},{6,8},{8,10},{10,12},{12,14},{14,16},{16,18},{18... | collective-permute-start | bytes 2359304 | tf_op jit(solution)/shard_map/ppermute | solution.py:17
  70.1 8.4 %collective-permute-start = (f32[3,1,4096]{2,1,0:T(1,128)}, f32[3,1,4096]{2,1,0:T(1,128)}, u32[]{:S(2)}, u32[]{:S(2)}) collective-permute-start(f32[3,1,4096]{2,1,0:T(1,128)} %get-tuple-element.465), channel_id=1, source_target_pairs={{0,1},{1,0},{2,3},{3,2},{4,5},{5,4},{6,7},{7,6},{8,9},{9,8},{10,11... | collective-permute-start | bytes 147464 | tf_op jit(solution)/shard_map/while/body/eval_jaxpr/ppermute | solution.py:27
  84.6 8.4 %collective-permute-start = (f32[3,1,4096]{2,1,0:T(1,128)}, f32[3,1,4096]{2,1,0:T(1,128)}, u32[]{:S(2)}, u32[]{:S(2)}) collective-permute-start(f32[3,1,4096]{2,1,0:T(1,128)} %get-tuple-element.465), channel_id=1, source_target_pairs={{0,1},{1,0},{2,3},{3,2},{4,5},{5,4},{6,7},{7,6},{8,9},{9,8},{10,11... | collective-permute-start | bytes 147464 | tf_op jit(solution)/shard_map/while/body/eval_jaxpr/ppermute | solution.py:27
  85.8 5.3 %collective-permute-start.1 = (f32[3,1,4096]{2,1,0:T(1,128)}, f32[3,1,4096]{2,1,0:T(1,128)}, u32[]{:S(2)}, u32[]{:S(2)}) collective-permute-start(f32[3,1,4096]{2,1,0:T(1,128)} %get-tuple-element.466), channel_id=1, source_target_pairs={{1,0},{0,1},{3,2},{2,3},{5,4},{4,5},{7,6},{6,7},{9,8},{8,9},{11,10... | collective-permute-start | bytes 147464 | tf_op jit(solution)/shard_map/while/body/eval_jaxpr/ppermute | solution.py:29
  98.4 18.3 %collective-permute-start.18 = (f32[3,16,4096]{2,1,0:T(8,128)S(1)}, f32[3,16,4096]{2,1,0:T(8,128)}, u32[]{:S(2)}, u32[]{:S(2)}) collective-permute-start(f32[3,16,4096]{2,1,0:T(8,128)S(1)} %get-tuple-element.65), channel_id=1, source_target_pairs={{0,4},{2,6},{4,8},{6,10},{8,12},{10,14},{12,16},{14,18},{16,20},{1... | collective-permute-start | bytes 2359304 | tf_op jit(solution)/shard_map/ppermute | solution.py:17
  119.8 8.4 %collective-permute-start.2 = (f32[3,1,4096]{2,1,0:T(1,128)}, f32[3,1,4096]{2,1,0:T(1,128)}, u32[]{:S(2)}, u32[]{:S(2)}) collective-permute-start(f32[3,1,4096]{2,1,0:T(1,128)} %get-tuple-element.494), channel_id=1, source_target_pairs={{0,1},{1,0},{2,3},{3,2},{4,5},{5,4},{6,7},{7,6},{8,9},{9,8},{10,11... | collective-permute-start | bytes 147464 | tf_op jit(solution)/shard_map/while/body/eval_jaxpr/ppermute | solution.py:27
  121.0 5.3 %collective-permute-start.3 = (f32[3,1,4096]{2,1,0:T(1,128)}, f32[3,1,4096]{2,1,0:T(1,128)}, u32[]{:S(2)}, u32[]{:S(2)}) collective-permute-start(f32[3,1,4096]{2,1,0:T(1,128)} %get-tuple-element.495), channel_id=1, source_target_pairs={{1,0},{0,1},{3,2},{2,3},{5,4},{4,5},{7,6},{6,7},{9,8},{8,9},{11,10... | collective-permute-start | bytes 147464 | tf_op jit(solution)/shard_map/while/body/eval_jaxpr/ppermute | solution.py:29
  134.3 8.4 %collective-permute-start.2 = (f32[3,1,4096]{2,1,0:T(1,128)}, f32[3,1,4096]{2,1,0:T(1,128)}, u32[]{:S(2)}, u32[]{:S(2)}) collective-permute-start(f32[3,1,4096]{2,1,0:T(1,128)} %get-tuple-element.494), channel_id=1, source_target_pairs={{0,1},{1,0},{2,3},{3,2},{4,5},{5,4},{6,7},{7,6},{8,9},{9,8},{10,11... | collective-permute-start | bytes 147464 | tf_op jit(solution)/shard_map/while/body/eval_jaxpr/ppermute | solution.py:27
  148.8 8.4 %collective-permute-start.2 = (f32[3,1,4096]{2,1,0:T(1,128)}, f32[3,1,4096]{2,1,0:T(1,128)}, u32[]{:S(2)}, u32[]{:S(2)}) collective-permute-start(f32[3,1,4096]{2,1,0:T(1,128)} %get-tuple-element.494), channel_id=1, source_target_pairs={{0,1},{1,0},{2,3},{3,2},{4,5},{5,4},{6,7},{7,6},{8,9},{9,8},{10,11... | collective-permute-start | bytes 147464 | tf_op jit(solution)/shard_map/while/body/eval_jaxpr/ppermute | solution.py:27
  163.3 8.4 %collective-permute-start.2 = (f32[3,1,4096]{2,1,0:T(1,128)}, f32[3,1,4096]{2,1,0:T(1,128)}, u32[]{:S(2)}, u32[]{:S(2)}) collective-permute-start(f32[3,1,4096]{2,1,0:T(1,128)} %get-tuple-element.494), channel_id=1, source_target_pairs={{0,1},{1,0},{2,3},{3,2},{4,5},{5,4},{6,7},{7,6},{8,9},{9,8},{10,11... | collective-permute-start | bytes 147464 | tf_op jit(solution)/shard_map/while/body/eval_jaxpr/ppermute | solution.py:27
  177.1 17.9 %collective-permute-start.19 = (f32[3,16,4096]{2,1,0:T(8,128)S(1)}, f32[3,16,4096]{2,1,0:T(8,128)S(1)}, u32[]{:S(2)}, u32[]{:S(2)}) collective-permute-start(f32[3,16,4096]{2,1,0:T(8,128)S(1)} %get-tuple-element.66), channel_id=1, source_target_pairs={{0,8},{2,10},{4,12},{6,14},{8,16},{10,18},{12,20},{14,22},{16,24},... | collective-permute-start | bytes 2359304 | tf_op jit(solution)/shard_map/ppermute | solution.py:17
  197.9 8.4 %collective-permute-start.4 = (f32[3,1,4096]{2,1,0:T(1,128)}, f32[3,1,4096]{2,1,0:T(1,128)}, u32[]{:S(2)}, u32[]{:S(2)}) collective-permute-start(f32[3,1,4096]{2,1,0:T(1,128)} %get-tuple-element.523), channel_id=1, source_target_pairs={{0,1},{1,0},{2,3},{3,2},{4,5},{5,4},{6,7},{7,6},{8,9},{9,8},{10,11... | collective-permute-start | bytes 147464 | tf_op jit(solution)/shard_map/while/body/eval_jaxpr/ppermute | solution.py:27
  198.9 5.7 %collective-permute-start.5 = (f32[3,1,4096]{2,1,0:T(1,128)}, f32[3,1,4096]{2,1,0:T(1,128)}, u32[]{:S(2)}, u32[]{:S(2)}) collective-permute-start(f32[3,1,4096]{2,1,0:T(1,128)} %get-tuple-element.524), channel_id=1, source_target_pairs={{1,0},{0,1},{3,2},{2,3},{5,4},{4,5},{7,6},{6,7},{9,8},{8,9},{11,10... | collective-permute-start | bytes 147464 | tf_op jit(solution)/shard_map/while/body/eval_jaxpr/ppermute | solution.py:29
  212.5 8.4 %collective-permute-start.4 = (f32[3,1,4096]{2,1,0:T(1,128)}, f32[3,1,4096]{2,1,0:T(1,128)}, u32[]{:S(2)}, u32[]{:S(2)}) collective-permute-start(f32[3,1,4096]{2,1,0:T(1,128)} %get-tuple-element.523), channel_id=1, source_target_pairs={{0,1},{1,0},{2,3},{3,2},{4,5},{5,4},{6,7},{7,6},{8,9},{9,8},{10,11... | collective-permute-start | bytes 147464 | tf_op jit(solution)/shard_map/while/body/eval_jaxpr/ppermute | solution.py:27
  213.4 5.7 %collective-permute-start.5 = (f32[3,1,4096]{2,1,0:T(1,128)}, f32[3,1,4096]{2,1,0:T(1,128)}, u32[]{:S(2)}, u32[]{:S(2)}) collective-permute-start(f32[3,1,4096]{2,1,0:T(1,128)} %get-tuple-element.524), channel_id=1, source_target_pairs={{1,0},{0,1},{3,2},{2,3},{5,4},{4,5},{7,6},{6,7},{9,8},{8,9},{11,10... | collective-permute-start | bytes 147464 | tf_op jit(solution)/shard_map/while/body/eval_jaxpr/ppermute | solution.py:29
  227.0 8.4 %collective-permute-start.4 = (f32[3,1,4096]{2,1,0:T(1,128)}, f32[3,1,4096]{2,1,0:T(1,128)}, u32[]{:S(2)}, u32[]{:S(2)}) collective-permute-start(f32[3,1,4096]{2,1,0:T(1,128)} %get-tuple-element.523), channel_id=1, source_target_pairs={{0,1},{1,0},{2,3},{3,2},{4,5},{5,4},{6,7},{7,6},{8,9},{9,8},{10,11... | collective-permute-start | bytes 147464 | tf_op jit(solution)/shard_map/while/body/eval_jaxpr/ppermute | solution.py:27
  227.9 5.7 %collective-permute-start.5 = (f32[3,1,4096]{2,1,0:T(1,128)}, f32[3,1,4096]{2,1,0:T(1,128)}, u32[]{:S(2)}, u32[]{:S(2)}) collective-permute-start(f32[3,1,4096]{2,1,0:T(1,128)} %get-tuple-element.524), channel_id=1, source_target_pairs={{1,0},{0,1},{3,2},{2,3},{5,4},{4,5},{7,6},{6,7},{9,8},{8,9},{11,10... | collective-permute-start | bytes 147464 | tf_op jit(solution)/shard_map/while/body/eval_jaxpr/ppermute | solution.py:29
  241.5 8.4 %collective-permute-start.4 = (f32[3,1,4096]{2,1,0:T(1,128)}, f32[3,1,4096]{2,1,0:T(1,128)}, u32[]{:S(2)}, u32[]{:S(2)}) collective-permute-start(f32[3,1,4096]{2,1,0:T(1,128)} %get-tuple-element.523), channel_id=1, source_target_pairs={{0,1},{1,0},{2,3},{3,2},{4,5},{5,4},{6,7},{7,6},{8,9},{9,8},{10,11... | collective-permute-start | bytes 147464 | tf_op jit(solution)/shard_map/while/body/eval_jaxpr/ppermute | solution.py:27
  242.4 5.7 %collective-permute-start.5 = (f32[3,1,4096]{2,1,0:T(1,128)}, f32[3,1,4096]{2,1,0:T(1,128)}, u32[]{:S(2)}, u32[]{:S(2)}) collective-permute-start(f32[3,1,4096]{2,1,0:T(1,128)} %get-tuple-element.524), channel_id=1, source_target_pairs={{1,0},{0,1},{3,2},{2,3},{5,4},{4,5},{7,6},{6,7},{9,8},{8,9},{11,10... | collective-permute-start | bytes 147464 | tf_op jit(solution)/shard_map/while/body/eval_jaxpr/ppermute | solution.py:29
  256.0 8.4 %collective-permute-start.4 = (f32[3,1,4096]{2,1,0:T(1,128)}, f32[3,1,4096]{2,1,0:T(1,128)}, u32[]{:S(2)}, u32[]{:S(2)}) collective-permute-start(f32[3,1,4096]{2,1,0:T(1,128)} %get-tuple-element.523), channel_id=1, source_target_pairs={{0,1},{1,0},{2,3},{3,2},{4,5},{5,4},{6,7},{7,6},{8,9},{9,8},{10,11... | collective-permute-start | bytes 147464 | tf_op jit(solution)/shard_map/while/body/eval_jaxpr/ppermute | solution.py:27
  256.9 5.7 %collective-permute-start.5 = (f32[3,1,4096]{2,1,0:T(1,128)}, f32[3,1,4096]{2,1,0:T(1,128)}, u32[]{:S(2)}, u32[]{:S(2)}) collective-permute-start(f32[3,1,4096]{2,1,0:T(1,128)} %get-tuple-element.524), channel_id=1, source_target_pairs={{1,0},{0,1},{3,2},{2,3},{5,4},{4,5},{7,6},{6,7},{9,8},{8,9},{11,10... | collective-permute-start | bytes 147464 | tf_op jit(solution)/shard_map/while/body/eval_jaxpr/ppermute | solution.py:29
  270.5 8.4 %collective-permute-start.4 = (f32[3,1,4096]{2,1,0:T(1,128)}, f32[3,1,4096]{2,1,0:T(1,128)}, u32[]{:S(2)}, u32[]{:S(2)}) collective-permute-start(f32[3,1,4096]{2,1,0:T(1,128)} %get-tuple-element.523), channel_id=1, source_target_pairs={{0,1},{1,0},{2,3},{3,2},{4,5},{5,4},{6,7},{7,6},{8,9},{9,8},{10,11... | collective-permute-start | bytes 147464 | tf_op jit(solution)/shard_map/while/body/eval_jaxpr/ppermute | solution.py:27
  271.4 5.7 %collective-permute-start.5 = (f32[3,1,4096]{2,1,0:T(1,128)}, f32[3,1,4096]{2,1,0:T(1,128)}, u32[]{:S(2)}, u32[]{:S(2)}) collective-permute-start(f32[3,1,4096]{2,1,0:T(1,128)} %get-tuple-element.524), channel_id=1, source_target_pairs={{1,0},{0,1},{3,2},{2,3},{5,4},{4,5},{7,6},{6,7},{9,8},{8,9},{11,10... | collective-permute-start | bytes 147464 | tf_op jit(solution)/shard_map/while/body/eval_jaxpr/ppermute | solution.py:29
  285.0 8.4 %collective-permute-start.4 = (f32[3,1,4096]{2,1,0:T(1,128)}, f32[3,1,4096]{2,1,0:T(1,128)}, u32[]{:S(2)}, u32[]{:S(2)}) collective-permute-start(f32[3,1,4096]{2,1,0:T(1,128)} %get-tuple-element.523), channel_id=1, source_target_pairs={{0,1},{1,0},{2,3},{3,2},{4,5},{5,4},{6,7},{7,6},{8,9},{9,8},{10,11... | collective-permute-start | bytes 147464 | tf_op jit(solution)/shard_map/while/body/eval_jaxpr/ppermute | solution.py:27
  285.9 5.7 %collective-permute-start.5 = (f32[3,1,4096]{2,1,0:T(1,128)}, f32[3,1,4096]{2,1,0:T(1,128)}, u32[]{:S(2)}, u32[]{:S(2)}) collective-permute-start(f32[3,1,4096]{2,1,0:T(1,128)} %get-tuple-element.524), channel_id=1, source_target_pairs={{1,0},{0,1},{3,2},{2,3},{5,4},{4,5},{7,6},{6,7},{9,8},{8,9},{11,10... | collective-permute-start | bytes 147464 | tf_op jit(solution)/shard_map/while/body/eval_jaxpr/ppermute | solution.py:29
  299.5 8.4 %collective-permute-start.4 = (f32[3,1,4096]{2,1,0:T(1,128)}, f32[3,1,4096]{2,1,0:T(1,128)}, u32[]{:S(2)}, u32[]{:S(2)}) collective-permute-start(f32[3,1,4096]{2,1,0:T(1,128)} %get-tuple-element.523), channel_id=1, source_target_pairs={{0,1},{1,0},{2,3},{3,2},{4,5},{5,4},{6,7},{7,6},{8,9},{9,8},{10,11... | collective-permute-start | bytes 147464 | tf_op jit(solution)/shard_map/while/body/eval_jaxpr/ppermute | solution.py:27
  300.5 5.7 %collective-permute-start.5 = (f32[3,1,4096]{2,1,0:T(1,128)}, f32[3,1,4096]{2,1,0:T(1,128)}, u32[]{:S(2)}, u32[]{:S(2)}) collective-permute-start(f32[3,1,4096]{2,1,0:T(1,128)} %get-tuple-element.524), channel_id=1, source_target_pairs={{1,0},{0,1},{3,2},{2,3},{5,4},{4,5},{7,6},{6,7},{9,8},{8,9},{11,10... | collective-permute-start | bytes 147464 | tf_op jit(solution)/shard_map/while/body/eval_jaxpr/ppermute | solution.py:29
  313.4 29.7 %collective-permute-start.20 = (f32[3,16,4096]{2,1,0:T(8,128)S(1)}, f32[3,16,4096]{2,1,0:T(8,128)S(1)}, u32[]{:S(2)}, u32[]{:S(2)}) collective-permute-start(f32[3,16,4096]{2,1,0:T(8,128)S(1)} %get-tuple-element.67), channel_id=1, source_target_pairs={{0,16},{2,18},{4,20},{6,22},{8,24},{10,26},{12,28},{14,30},{1,17},... | collective-permute-start | bytes 2359304 | tf_op jit(solution)/shard_map/ppermute | solution.py:17
  344.3 13.3 %collective-permute-start.21 = (f32[3,16,4096]{2,1,0:T(8,128)S(1)}, f32[3,16,4096]{2,1,0:T(8,128)S(1)}, u32[]{:S(2)}, u32[]{:S(2)}) collective-permute-start(f32[3,16,4096]{2,1,0:T(8,128)S(1)} %add.572), channel_id=1, source_target_pairs={{0,2},{2,4},{4,6},{6,8},{8,10},{10,12},{12,14},{14,16},{16,18},{18... | collective-permute-start | bytes 2359304 | tf_op jit(solution)/shard_map/ppermute | solution.py:17
  (126 other events, 323.9 us)
where the time goes:
time: 365 us; the launch traced here: 359 us
  local copies, waits for them, and re-layouts  119 us (33%)
  waiting for transfers between devices  103 us (28%)
  other arithmetic  86.4 us (24%)
  starting transfers between devices  48.6 us (13%)
    ppermute x6, waiting for transfers between devices, from_behind(): return lax.ppermute(value, axis, pairs)  87.5 us
    slice x38, local copies, waits for them, and re-layouts, diffuse(): jnp.roll(centre, 1, -1)  29.3 us
    concatenate x72, local copies, waits for them, and re-layouts, diffuse(): jnp.roll(centre, 1, -1)  26.4 us
    concatenate x14, local copies, waits for them, and re-layouts, extended(): jnp.concatenate([lax.ppermute(tail, axis, [(i, (i + 1) % count) for i in...  25.6 us
    add x18, other arithmetic, tendency(): -column_slope(height_c) + coriolis * north_c  23.4 us
    ppermute x19, starting transfers between devices, extended(): lax.ppermute(head, axis, [((i + 1) % count, i) for i in range(count)])  20.1 us
    while x210, local copies, waits for them, and re-layouts  19.2 us
    ppermute x19, starting transfers between devices, extended(): lax.ppermute(tail, axis, [(i, (i + 1) % count) for i in range(count)])  18.7 us
  transfers between devices with their start and end apart: 44, of which 16 were waited for; matrix products, arithmetic and copies ran while one was open for 27% of the time, Pallas kernels for 0%

commit v1 on v0

v1 whole, which is shorter than its diff:
```python
import functools

import jax
import jax.numpy as jnp
from jax import lax
from jax.experimental import pallas as pl
from jax.experimental.pallas import tpu as pltpu
from jax.sharding import PartitionSpec as P

MESH = pl.DeviceIdType.MESH
DT = 0.3
NU = 1.0 / 3.0
FC = 0.5
LANES = 128
GROUPS = 4


def shift_left(v):
    return pltpu.roll(v, v.shape[1] - 1, 1)


def shift_right(v):
    return pltpu.roll(v, 1, 1)


def shift_up(v):
    return pltpu.roll(v, v.shape[0] - 1, 0)


def shift_down(v):
    return pltpu.roll(v, 1, 0)


def row_terms(h, e, n, depth):
    dn = 0.5 * (depth * n)
    nh, ne, nn, hh = NU * h, NU * e, NU * n, 0.5 * h
    return (nh - dn, ne, nn - hh), (nh + dn, ne, nn + hh)


def column_terms(h, e, n, depth):
    de = 0.5 * (depth * e)
    nh, ne, nn, hh = NU * h, NU * e, NU * n, 0.5 * h
    return (
        shift_left(nh - de) + shift_right(nh + de) - 4.0 * nh,
        shift_left(ne - hh) + shift_right(ne + hh) - 4.0 * ne + FC * n,
        shift_left(nn) + shift_right(nn) - 4.0 * nn - FC * e,
    )


def kernel(
    cfg, u_ref, init_ref, depth_ref, out_ref,
    s0, g, s1, mid, b, halo_src, dsrc, dep, main, halo, cs, ce, cb, esrc, edst,
    shift_s, shift_r, edge_s, edge_r, dep_s, dep_r, a2a_s, a2a_r, ret_s, ret_r, fwd_s, fwd_r,
):
    T, SP, RL, NX, W, K, stride, hw, per, nh = cfg
    p, y = lax.axis_index("tm"), lax.axis_index("space")
    me = p * SP + y
    total = T * SP
    mine = me // stride
    is_owner = lax.rem(me, stride) == 0

    def where(flat):
        return (flat // SP, lax.rem(flat, SP))

    barrier = pltpu.get_barrier_semaphore()

    @pl.loop(1, total)
    def _(i):
        pl.semaphore_signal(barrier, inc=1, device_id=where(lax.rem(me + i, total)), device_id_type=MESH)

    pl.semaphore_wait(barrier, total - 1)

    shift = pltpu.make_async_remote_copy(
        src_ref=u_ref.at[0, 2], dst_ref=s0, send_sem=shift_s, recv_sem=shift_r,
        device_id=(lax.rem(p + 1, T), y), device_id_type=MESH,
    )

    @pl.when(p < T - 1)
    def _():
        shift.start()

    lane_h = lax.broadcasted_iota(jnp.int32, (RL, LANES), 1)

    def dep_copy(yo):
        return pltpu.make_async_remote_copy(
            src_ref=dsrc.at[yo], dst_ref=dep.at[pl.ds(pl.multiple_of(y * RL, 8), RL)],
            send_sem=dep_s.at[yo], recv_sem=dep_r, device_id=(p, yo), device_id_type=MESH,
        )

    for yo in range(SP):
        flat = p * SP + yo
        k = flat // stride

        @pl.when(lax.rem(flat, stride) == 0)
        def _():
            here = depth_ref[:, pl.ds(pl.multiple_of(k * W, LANES), W)]
            after = depth_ref[:, pl.ds(pl.multiple_of(lax.rem((k + 1) * W, NX), LANES), LANES)]
            before = depth_ref[:, pl.ds(pl.multiple_of(lax.rem(k * W + NX - LANES, NX), LANES), LANES)]
            dsrc[yo, :, :W] = here
            dsrc[yo, :, W:] = jnp.where(lane_h < LANES // 2, after, before)

            @pl.when(yo != y)
            def _():
                dep_copy(yo).start()

            @pl.when(yo == y)
            def _():
                pltpu.make_async_copy(
                    dsrc.at[yo], dep.at[pl.ds(pl.multiple_of(y * RL, 8), RL)], dep_r
                ).start()

    for f in range(3):
        g[f] = (-7.0 / 24.0) * u_ref[0, 0, f] + (1.0 / 3.0) * u_ref[0, 1, f] - (1.0 / 24.0) * u_ref[0, 2, f]

    @pl.when(p > 0)
    def _():
        shift.wait_recv()

    @pl.when(p == 0)
    def _():
        s0[...] = init_ref[...]

    for f in range(3):
        g[f] = g[f] + 0.5 * s0[f]

    row = lax.broadcasted_iota(jnp.int32, (RL, NX), 0)

    def edge_copy(stage, side):
        to = lax.rem(y + SP - 1, SP) if side == 0 else lax.rem(y + 1, SP)
        return pltpu.make_async_remote_copy(
            src_ref=esrc.at[stage, side], dst_ref=edst.at[stage, side],
            send_sem=edge_s.at[stage, side], recv_sem=edge_r.at[stage, side],
            device_id=(p, to), device_id_type=MESH,
        )

    def rate_of_g(stage):
        up0, _ = row_terms(g[0, 0:1], g[1, 0:1], g[2, 0:1], depth_ref[0:1])
        _, down1 = row_terms(g[0, RL - 1 : RL], g[1, RL - 1 : RL], g[2, RL - 1 : RL], depth_ref[RL - 1 : RL])
        for f in range(3):
            esrc[stage, 0, f] = up0[f]
            esrc[stage, 1, f] = down1[f]
        for side in range(2):
            edge_copy(stage, side).start()
        h, e, n, depth = g[0], g[1], g[2], depth_ref[...]
        rates = column_terms(h, e, n, depth)
        ups, downs = row_terms(h, e, n, depth)
        for side in range(2):
            edge_copy(stage, side).wait_recv()
        return [
            rates[f]
            + jnp.where(row == RL - 1, edst[stage, 0, f], shift_up(ups[f]))
            + jnp.where(row == 0, edst[stage, 1, f], shift_down(downs[f]))
            for f in range(3)
        ]

    rates = rate_of_g(0)
    for f in range(3):
        s1[f] = s0[f] + DT * rates[f]
    for f in range(3):
        g[f] = (
            0.5 * s1[f]
            - (1.0 / 24.0) * u_ref[0, 0, f] - (1.0 / 6.0) * u_ref[0, 1, f] + (5.0 / 24.0) * u_ref[0, 2, f]
        )
    rates = rate_of_g(1)
    first = jnp.where(p == 0, 1.0, 0.0).astype(jnp.float32)
    for f in range(3):
        s2 = s1[f] + DT * rates[f]
        g[f] = (1.0 / 6.0) * s2 + (2.0 / 3.0) * s1[f] + (first - 5.0 / 6.0) * s0[f]
        mid[f] = s1[f] - 0.5 * (s0[f] + s2)
    rates = rate_of_g(2)
    for f in range(3):
        b[f] = first * s0[f] + DT * rates[f]

    slot_of = lax.rem(lane_h + hw, LANES) // (2 * hw)
    for k in range(K):
        lo, hi = ((k + 1) % K) * W, (k * W - LANES) % NX
        packed = [jnp.zeros((RL, LANES), jnp.float32) for _ in range(nh)]
        for f in range(3):
            z = jnp.where(lane_h < LANES // 2, b[f, :, lo : lo + LANES], b[f, :, hi : hi + LANES])
            slot = f % per
            if slot:
                z = pltpu.roll(z, 2 * hw * slot, 1)
            packed[f // per] = jnp.where(slot_of == slot, z, packed[f // per])
        for i in range(nh):
            halo_src[i, :, k * LANES : (k + 1) * LANES] = packed[i]

    my_rows = pl.ds(pl.multiple_of(y * RL, 8), RL)

    def a2a(k):
        ends = (
            (b.at[:, :, pl.ds(pl.multiple_of(k * W, LANES), W)], main.at[p, :, my_rows]),
            (halo_src.at[:, :, pl.ds(pl.multiple_of(k * LANES, LANES), LANES)], halo.at[p, :, my_rows]),
        )
        there = [
            pltpu.make_async_remote_copy(
                src_ref=src, dst_ref=dst, send_sem=a2a_s.at[i], recv_sem=a2a_r.at[i, p],
                device_id=where(k * stride), device_id_type=MESH,
            )
            for i, (src, dst) in enumerate(ends)
        ]
        here = [pltpu.make_async_copy(src, dst, a2a_r.at[i, p]) for i, (src, dst) in enumerate(ends)]
        return there, here

    @pl.loop(0, K)
    def _(i):
        k = lax.rem(mine + i, K)
        there, here = a2a(k)

        @pl.when(k * stride != me)
        def _():
            for copy in there:
                copy.start()

        @pl.when(k * stride == me)
        def _():
            for copy in here:
                copy.start()

    my_tile = pl.ds(pl.multiple_of(mine * W, LANES), W)
    my_group = mine // (K // GROUPS)

    def give_back(t):
        for yo in range(SP):
            src, dst = cs.at[t * SP + yo], ce.at[:, :, my_tile]
            here = jnp.logical_and(t == p, y == yo)

            @pl.when(jnp.logical_not(here))
            def _():
                pltpu.make_async_remote_copy(
                    src_ref=src, dst_ref=dst, send_sem=ret_s, recv_sem=ret_r.at[my_group],
                    device_id=(t, yo), device_id_type=MESH,
                ).start()

            @pl.when(here)
            def _():
                pltpu.make_async_copy(src, dst, ret_r.at[my_group]).start()

    def whole(ref, sem):
        pltpu.make_async_copy(ref, ref, sem).wait()

    @pl.when(is_owner)
    def _():
        whole(dep, dep_r)
        depth = dep[...]

        def turn(t, cur):
            h, e, n = cur
            rates = column_terms(h, e, n, depth)
            ups, downs = row_terms(h, e, n, depth)
            whole(main.at[t], a2a_r.at[0, t])
            whole(halo.at[t], a2a_r.at[1, t])
            new = []
            for f in range(3):
                tile = halo[t, f // per]
                if f % per:
                    tile = pltpu.roll(tile, LANES - 2 * hw * (f % per), 1)
                window = jnp.concatenate([main[t, f], tile], axis=1)
                value = window + cur[f] + DT * (rates[f] + shift_up(ups[f]) + shift_down(downs[f]))
                for yo in range(SP):
                    cs[t * SP + yo, f] = value[yo * RL : (yo + 1) * RL, :W]
                new.append(value)

            @pl.when(t > 0)
            def _():
                give_back(t - 1)

            return tuple(new)

        zero = jnp.zeros(dep.shape, jnp.float32)
        lax.fori_loop(0, T, turn, (zero, zero, zero))
        give_back(T - 1)

    width = NX // GROUPS

    def fwd(q):
        cols = pl.ds(q * width, width)
        return pltpu.make_async_remote_copy(
            src_ref=ce.at[:, :, cols], dst_ref=cb.at[:, :, cols],
            send_sem=fwd_s.at[q], recv_sem=fwd_r.at[q], device_id=(lax.rem(p + 1, T), y), device_id_type=MESH,
        )

    for q in range(GROUPS):
        whole(ce.at[:, :, pl.ds(q * width, width)], ret_r.at[q])

        @pl.when(p < T - 1)
        def _():
            fwd(q).start()

    @pl.when(p == 0)
    def _():
        cb[...] = init_ref[...]

    for q in range(GROUPS):
        @pl.when(p > 0)
        def _():
            fwd(q).wait_recv()

        cols = pl.ds(q * width, width)
        for f in range(3):
            start, end = cb[f, :, cols], ce[f, :, cols]
            out_ref[0, 0, f, :, cols] = start
            out_ref[0, 1, f, :, cols] = mid[f, :, cols] + 0.5 * (start + end)
            out_ref[0, 2, f, :, cols] = end

    @pl.when(p < T - 1)
    def _():
        shift.wait_send()
        for q in range(GROUPS):
            fwd(q).wait_send()

    for stage in range(3):
        for side in range(2):
            edge_copy(stage, side).wait_send()
    for yo in range(SP):
        flat = p * SP + yo

        @pl.when(jnp.logical_and(lax.rem(flat, stride) == 0, yo != y))
        def _():
            dep_copy(yo).wait_send()

    @pl.when(is_owner)
    def _():
        whole(b.at[:, :, pl.ds(0, (K - 1) * W)], a2a_s.at[0])
        whole(halo_src.at[:, :, pl.ds(0, (K - 1) * LANES)], a2a_s.at[1])
        whole(cs.at[pl.ds(0, total - 1)], ret_s)

    @pl.when(jnp.logical_not(is_owner))
    def _():
        whole(b, a2a_s.at[0])
        whole(halo_src, a2a_s.at[1])


def solution(mesh):
    T, SP = mesh.shape["tm"], mesh.shape["space"]

    def per_device(fine_nodes, init_state, mean_depth):
        RL, NX = mean_depth.shape
        total = T * SP
        W = max(LANES, NX // total)
        K = NX // W
        stride = total // K
        hw = 8
        while hw < T:
            hw *= 2
        per = LANES // (2 * hw)
        nh = -(-3 // per)
        cfg = (T, SP, RL, NX, W, K, stride, hw, per, nh)
        f32, dma = jnp.float32, pltpu.SemaphoreType.DMA
        state = pltpu.VMEM((3, RL, NX), f32)
        R = RL * SP
        vmem = pl.BlockSpec(memory_space=pltpu.VMEM)
        return pl.pallas_call(
            functools.partial(kernel, cfg),
            out_shape=jax.ShapeDtypeStruct(fine_nodes.shape, f32),
            in_specs=[vmem] * 3,
            out_specs=vmem,
            scratch_shapes=[
                state, state, state, state, state,
                pltpu.VMEM((nh, RL, K * LANES), f32),
                pltpu.VMEM((SP, RL, W + LANES), f32),
                pltpu.VMEM((R, W + LANES), f32),
                pltpu.VMEM((T, 3, R, W), f32),
                pltpu.VMEM((T, nh, R, LANES), f32),
                pltpu.VMEM((total, 3, RL, W), f32),
                state, state,
                pltpu.VMEM((3, 2, 3, 1, NX), f32),
                pltpu.VMEM((3, 2, 3, 1, NX), f32),
                dma, dma, dma((3, 2)), dma((3, 2)), dma((SP,)), dma, dma((2,)), dma((2, T)),
                dma, dma((GROUPS,)), dma((GROUPS,)), dma((GROUPS,)),
            ],
            compiler_params=pltpu.CompilerParams(
                collective_id=0, has_side_effects=True, vmem_limit_bytes=60 * 1024 * 1024
            ),
        )(fine_nodes, init_state, mean_depth)

    return jax.shard_map(
        per_device,
        mesh=mesh,
        in_specs=(P("tm", None, None, "space", None), P(None, "space", None), P("space", None)),
        out_specs=P("tm", None, None, "space", None),
        check_vma=False,
    )
```

time: 365 us -> 81.4 us (0.22)
  the two profiles are of different devices: /device:TPU:26 before, /device:TPU:16 now
where the time goes in v1:
time: 81.4 us; the launch traced here: 81.2 us
  Pallas kernels  77.9 us (96%)
  local copies, waits for them, and re-layouts  3.27 us (4%)
    pallas_call x1, Pallas kernels, per_device(): pl.pallas_call(functools.partial(kernel, cfg), out_shape=jax.ShapeDtypeSt...  77.9 us
    unnamed x1, local copies, waits for them, and re-layouts  3.27 us

profile of v1, /device:TPU:16, one launch (start us, length us, event | category | flops | bytes accessed | tf_op | source)
XLA Modules:
  0.0 81.2 jit_solution(2994370720980989378)
XLA Ops:
  0.0 77.9 %shard_map.37 = f32[1,3,3,16,4096]{4,3,2,1,0:T(8,128)} custom-call(f32[1,3,3,16,4096]{4,3,2,1,0:T(8,128)} %u_ref.1, f32[3,16,4096]{2,1,0:T(8,128)} %init_ref.1, f32[16,4096]{1,0:T(8,128)} %depth_ref.1), custom_call_target="tpu_custom_call" | custom-call | tf_op jit(solution)/shard_map/pallas_call | solution.py:352
  77.9 3.3 %copy.5 = f32[1,3,3,16,4096]{4,3,2,1,0:T(8,128)} copy(f32[1,3,3,16,4096]{4,3,2,1,0:T(8,128)} %shard_map.37) | data formatting | bytes 4718592

commit v2 on v1

--- a/solution.py
+++ b/solution.py
@@ -49,15 +49,21 @@
 
 def kernel(
     cfg, u_ref, init_ref, depth_ref, out_ref,
-    s0, g, s1, mid, b, halo_src, dsrc, dep, main, halo, cs, ce, cb, esrc, edst,
+    s0, g, s1, mid, b, halo_src, dsrc, dep, main, halo, cs, ce, cb, esrc, edst, cin, chalo, chalo_src,
     shift_s, shift_r, edge_s, edge_r, dep_s, dep_r, a2a_s, a2a_r, ret_s, ret_r, fwd_s, fwd_r,
+    c_s, c_r, beg_s, beg_r,
 ):
-    T, SP, RL, NX, W, K, stride, hw, per, nh = cfg
+    T, SP, RL, NX, W, K, stride, hw, per, nh, NG = cfg
+    TG = T // NG
     p, y = lax.axis_index("tm"), lax.axis_index("space")
     me = p * SP + y
     total = T * SP
-    mine = me // stride
-    is_owner = lax.rem(me, stride) == 0
+    block = p // TG
+    pb = p - block * TG
+    local = pb * SP + y
+    mine = local // stride
+    is_owner = lax.rem(local, stride) == 0
+    even = lax.rem(p, 2) == 0
 
     def where(flat):
         return (flat // SP, lax.rem(flat, SP))
@@ -88,7 +94,7 @@
         )
 
     for yo in range(SP):
-        flat = p * SP + yo
+        flat = pb * SP + yo
         k = flat // stride
 
         @pl.when(lax.rem(flat, stride) == 0)
@@ -188,17 +194,17 @@
 
     def a2a(k):
         ends = (
-            (b.at[:, :, pl.ds(pl.multiple_of(k * W, LANES), W)], main.at[p, :, my_rows]),
-            (halo_src.at[:, :, pl.ds(pl.multiple_of(k * LANES, LANES), LANES)], halo.at[p, :, my_rows]),
+            (b.at[:, :, pl.ds(pl.multiple_of(k * W, LANES), W)], main.at[pb, :, my_rows]),
+            (halo_src.at[:, :, pl.ds(pl.multiple_of(k * LANES, LANES), LANES)], halo.at[pb, :, my_rows]),
         )
         there = [
             pltpu.make_async_remote_copy(
-                src_ref=src, dst_ref=dst, send_sem=a2a_s.at[i], recv_sem=a2a_r.at[i, p],
-                device_id=where(k * stride), device_id_type=MESH,
+                src_ref=src, dst_ref=dst, send_sem=a2a_s.at[i], recv_sem=a2a_r.at[i, pb],
+                device_id=where(block * TG * SP + k * stride), device_id_type=MESH,
             )
             for i, (src, dst) in enumerate(ends)
         ]
-        here = [pltpu.make_async_copy(src, dst, a2a_r.at[i, p]) for i, (src, dst) in enumerate(ends)]
+        here = [pltpu.make_async_copy(src, dst, a2a_r.at[i, pb]) for i, (src, dst) in enumerate(ends)]
         return there, here
 
     @pl.loop(0, K)
@@ -206,12 +212,12 @@
         k = lax.rem(mine + i, K)
         there, here = a2a(k)
 
-        @pl.when(k * stride != me)
+        @pl.when(k * stride != local)
         def _():
             for copy in there:
                 copy.start()
 
-        @pl.when(k * stride == me)
+        @pl.when(k * stride == local)
         def _():
             for copy in here:
                 copy.start()
@@ -222,18 +228,54 @@
     def give_back(t):
         for yo in range(SP):
             src, dst = cs.at[t * SP + yo], ce.at[:, :, my_tile]
-            here = jnp.logical_and(t == p, y == yo)
+            here = jnp.logical_and(t == pb, y == yo)
 
             @pl.when(jnp.logical_not(here))
             def _():
                 pltpu.make_async_remote_copy(
                     src_ref=src, dst_ref=dst, send_sem=ret_s, recv_sem=ret_r.at[my_group],
-                    device_id=(t, yo), device_id_type=MESH,
+                    device_id=(block * TG + t, yo), device_id_type=MESH,
                 ).start()
 
             @pl.when(here)
             def _():
                 pltpu.make_async_copy(src, dst, ret_r.at[my_group]).start()
+
+    def give_begin(t, src):
+        for yo in range(SP):
+            dst = cb.at[:, :, my_tile]
+            here = jnp.logical_and(t == pb, y == yo)
+
+            @pl.when(jnp.logical_not(here))
+            def _():
+                pltpu.make_async_remote_copy(
+                    src_ref=src.at[yo], dst_ref=dst, send_sem=beg_s.at[t * SP + yo], recv_sem=beg_r,
+                    device_id=(block * TG + t, yo), device_id_type=MESH,
+                ).start()
+
+            @pl.when(here)
+            def _():
+                pltpu.make_async_copy(src.at[yo], dst, beg_r).start()
+
+    def give(t):
+        give_back(t)
+
+        @pl.when(jnp.logical_and(lax.rem(t, 2) == 1, t < TG - 1))
+        def _():
+            give_begin(t + 1, cs.at[pl.ds(t * SP, SP)])
+
+    def carry():
+        ends = ((cs.at[pl.ds((TG - 1) * SP, SP)], cin), (chalo_src, chalo))
+        return [
+            pltpu.make_async_remote_copy(
+                src_ref=src, dst_ref=dst, send_sem=c_s.at[i], recv_sem=c_r.at[i],
+                device_id=(lax.rem(p + TG, T), y), device_id_type=MESH,
+            )
+            for i, (src, dst) in enumerate(ends)
+        ]
+
+    def unpack(tile, f):
+        return pltpu.roll(tile, LANES - 2 * hw * (f % per), 1) if f % per else tile
 
     def whole(ref, sem):
         pltpu.make_async_copy(ref, ref, sem).wait()
@@ -251,24 +293,59 @@
             whole(halo.at[t], a2a_r.at[1, t])
             new = []
             for f in range(3):
-                tile = halo[t, f // per]
-                if f % per:
-                    tile = pltpu.roll(tile, LANES - 2 * hw * (f % per), 1)
-                window = jnp.concatenate([main[t, f], tile], axis=1)
+                window = jnp.concatenate([main[t, f], unpack(halo[t, f // per], f)], axis=1)
                 value = window + cur[f] + DT * (rates[f] + shift_up(ups[f]) + shift_down(downs[f]))
                 for yo in range(SP):
                     cs[t * SP + yo, f] = value[yo * RL : (yo + 1) * RL, :W]
                 new.append(value)
 
-            @pl.when(t > 0)
-            def _():
-                give_back(t - 1)
+            @pl.when(jnp.logical_and(t > 0, block == NG - 1))
+            def _():
+                give(t - 1)
 
             return tuple(new)
 
-        zero = jnp.zeros(dep.shape, jnp.float32)
-        lax.fori_loop(0, T, turn, (zero, zero, zero))
-        give_back(T - 1)
+        @pl.when(block == 0)
+        def _():
+            cin[...] = jnp.zeros_like(cin)
+            chalo[...] = jnp.zeros_like(chalo)
+
+        @pl.when(block > 0)
+        def _():
+            for copy in carry():
+                copy.wait_recv()
+            give_begin(0, cin)
+
+        first_state = tuple(
+            jnp.concatenate(
+                [jnp.concatenate([cin[yo, f] for yo in range(SP)], axis=0), unpack(chalo[f // per], f)], axis=1
+            )
+            for f in range(3)
+        )
+        last = lax.fori_loop(0, TG, turn, first_state)
+
+        @pl.when(block == NG - 1)
+        def _():
+            give(TG - 1)
+
+        @pl.when(block < NG - 1)
+        def _():
+            lanes = lax.broadcasted_iota(jnp.int32, (SP * RL, LANES), 1)
+            slots = lax.rem(lanes + hw, LANES) // (2 * hw)
+            for i in range(nh):
+                packed = jnp.zeros((SP * RL, LANES), jnp.float32)
+                for f in range(i * per, min(3, (i + 1) * per)):
+                    z = last[f][:, W:]
+                    if f % per:
+                        z = pltpu.roll(z, 2 * hw * (f % per), 1)
+                    packed = jnp.where(slots == f % per, z, packed)
+                chalo_src[i] = packed
+            for copy in carry():
+                copy.start()
+
+            @pl.loop(0, TG)
+            def _(t):
+                give(t)
 
     width = NX // GROUPS
 
@@ -282,7 +359,7 @@
     for q in range(GROUPS):
         whole(ce.at[:, :, pl.ds(q * width, width)], ret_r.at[q])
 
-        @pl.when(p < T - 1)
+        @pl.when(even)
         def _():
             fwd(q).start()
 
@@ -290,8 +367,12 @@
     def _():
         cb[...] = init_ref[...]
 
+    @pl.when(jnp.logical_and(even, p > 0))
+    def _():
+        whole(cb, beg_r)
+
     for q in range(GROUPS):
-        @pl.when(p > 0)
+        @pl.when(jnp.logical_not(even))
         def _():
             fwd(q).wait_recv()
 
@@ -305,6 +386,9 @@
     @pl.when(p < T - 1)
     def _():
         shift.wait_send()
+
+    @pl.when(even)
+    def _():
         for q in range(GROUPS):
             fwd(q).wait_send()
 
@@ -312,7 +396,7 @@
         for side in range(2):
             edge_copy(stage, side).wait_send()
     for yo in range(SP):
-        flat = p * SP + yo
+        flat = pb * SP + yo
 
         @pl.when(jnp.logical_and(lax.rem(flat, stride) == 0, yo != y))
         def _():
@@ -322,7 +406,22 @@
     def _():
         whole(b.at[:, :, pl.ds(0, (K - 1) * W)], a2a_s.at[0])
         whole(halo_src.at[:, :, pl.ds(0, (K - 1) * LANES)], a2a_s.at[1])
-        whole(cs.at[pl.ds(0, total - 1)], ret_s)
+        whole(cs.at[pl.ds(0, TG * SP - 1)], ret_s)
+
+        @pl.when(block < NG - 1)
+        def _():
+            for copy in carry():
+                copy.wait_send()
+
+        for t in range(0, TG, 2):
+            for yo in range(SP):
+                sent = jnp.logical_not(jnp.logical_and(t == pb, y == yo))
+                if t == 0:
+                    sent = jnp.logical_and(sent, block > 0)
+
+                @pl.when(sent)
+                def _():
+                    pltpu.make_async_copy(cin.at[yo], cin.at[yo], beg_s.at[t * SP + yo]).wait()
 
     @pl.when(jnp.logical_not(is_owner))
     def _():
@@ -335,16 +434,17 @@
 
     def per_device(fine_nodes, init_state, mean_depth):
         RL, NX = mean_depth.shape
-        total = T * SP
-        W = max(LANES, NX // total)
+        NG = 2 if T % 4 == 0 else 1
+        members = T // NG * SP
+        W = max(LANES, NX // members)
         K = NX // W
-        stride = total // K
+        stride = members // K
         hw = 8
         while hw < T:
             hw *= 2
         per = LANES // (2 * hw)
         nh = -(-3 // per)
-        cfg = (T, SP, RL, NX, W, K, stride, hw, per, nh)
+        cfg = (T, SP, RL, NX, W, K, stride, hw, per, nh, NG)
         f32, dma = jnp.float32, pltpu.SemaphoreType.DMA
         state = pltpu.VMEM((3, RL, NX), f32)
         R = RL * SP
@@ -359,14 +459,18 @@
                 pltpu.VMEM((nh, RL, K * LANES), f32),
                 pltpu.VMEM((SP, RL, W + LANES), f32),
                 pltpu.VMEM((R, W + LANES), f32),
-                pltpu.VMEM((T, 3, R, W), f32),
-                pltpu.VMEM((T, nh, R, LANES), f32),
-                pltpu.VMEM((total, 3, RL, W), f32),
+                pltpu.VMEM((T // NG, 3, R, W), f32),
+                pltpu.VMEM((T // NG, nh, R, LANES), f32),
+                pltpu.VMEM((members, 3, RL, W), f32),
                 state, state,
                 pltpu.VMEM((3, 2, 3, 1, NX), f32),
                 pltpu.VMEM((3, 2, 3, 1, NX), f32),
-                dma, dma, dma((3, 2)), dma((3, 2)), dma((SP,)), dma, dma((2,)), dma((2, T)),
+                pltpu.VMEM((SP, 3, RL, W), f32),
+                pltpu.VMEM((nh, R, LANES), f32),
+                pltpu.VMEM((nh, R, LANES), f32),
+                dma, dma, dma((3, 2)), dma((3, 2)), dma((SP,)), dma, dma((2,)), dma((2, T // NG)),
                 dma, dma((GROUPS,)), dma((GROUPS,)), dma((GROUPS,)),
+                dma((2,)), dma((2,)), dma((members,)), dma,
             ],
             compiler_params=pltpu.CompilerParams(
                 collective_id=0, has_side_effects=True, vmem_limit_bytes=60 * 1024 * 1024

time: 81.4 us -> 68.5 us (0.84)
  the two profiles are of different devices: /device:TPU:16 before, /device:TPU:27 now
where the time goes in v2:
time: 68.5 us; the launch traced here: 68.3 us
  Pallas kernels  65.1 us (95%)
  local copies, waits for them, and re-layouts  3.27 us (5%)
    pallas_call x1, Pallas kernels, per_device(): pl.pallas_call(functools.partial(kernel, cfg), out_shape=jax.ShapeDtypeSt...  65.1 us
    unnamed x1, local copies, waits for them, and re-layouts  3.27 us

profile of v2, /device:TPU:27, one launch (start us, length us, event | category | flops | bytes accessed | tf_op | source)
XLA Modules:
  0.0 68.3 jit_solution(10077508698485814025)
XLA Ops:
  0.0 65.1 %shard_map.37 = f32[1,3,3,16,4096]{4,3,2,1,0:T(8,128)} custom-call(f32[1,3,3,16,4096]{4,3,2,1,0:T(8,128)} %u_ref.1, f32[3,16,4096]{2,1,0:T(8,128)} %init_ref.1, f32[16,4096]{1,0:T(8,128)} %depth_ref.1), custom_call_target="tpu_custom_call" | custom-call | tf_op jit(solution)/shard_map/pallas_call | solution.py:452
  65.1 3.3 %copy.5 = f32[1,3,3,16,4096]{4,3,2,1,0:T(8,128)} copy(f32[1,3,3,16,4096]{4,3,2,1,0:T(8,128)} %shard_map.37) | data formatting | bytes 4718592

commit v3 on v2

--- a/solution.py
+++ b/solution.py
@@ -48,10 +48,10 @@
 
 
 def kernel(
-    cfg, u_ref, init_ref, depth_ref, out_ref,
+    cfg, u_hbm, init_hbm, depth_hbm, out_ref, u_ref, init_ref, depth_ref,
     s0, g, s1, mid, b, halo_src, dsrc, dep, main, halo, cs, ce, cb, esrc, edst, cin, chalo, chalo_src,
     shift_s, shift_r, edge_s, edge_r, dep_s, dep_r, a2a_s, a2a_r, ret_s, ret_r, fwd_s, fwd_r,
-    c_s, c_r, beg_s, beg_r,
+    c_s, c_r, beg_s, beg_r, in_s,
 ):
     T, SP, RL, NX, W, K, stride, hw, per, nh, NG = cfg
     TG = T // NG
@@ -74,16 +74,25 @@
     def _(i):
         pl.semaphore_signal(barrier, inc=1, device_id=where(lax.rem(me + i, total)), device_id_type=MESH)
 
+    loads = [pltpu.make_async_copy(u_hbm.at[0, i], u_ref.at[i], in_s.at[i]) for i in (2, 0, 1)]
+    loads.append(pltpu.make_async_copy(depth_hbm, depth_ref, in_s.at[3]))
+    loads.append(pltpu.make_async_copy(init_hbm, init_ref, in_s.at[4]))
+    for copy in loads:
+        copy.start()
+    loads[0].wait()
     pl.semaphore_wait(barrier, total - 1)
 
     shift = pltpu.make_async_remote_copy(
-        src_ref=u_ref.at[0, 2], dst_ref=s0, send_sem=shift_s, recv_sem=shift_r,
+        src_ref=u_ref.at[2], dst_ref=s0, send_sem=shift_s, recv_sem=shift_r,
         device_id=(lax.rem(p + 1, T), y), device_id_type=MESH,
     )
 
     @pl.when(p < T - 1)
     def _():
         shift.start()
+
+    for copy in loads[1:]:
+        copy.wait()
 
     lane_h = lax.broadcasted_iota(jnp.int32, (RL, LANES), 1)
 
@@ -116,7 +125,7 @@
                 ).start()
 
     for f in range(3):
-        g[f] = (-7.0 / 24.0) * u_ref[0, 0, f] + (1.0 / 3.0) * u_ref[0, 1, f] - (1.0 / 24.0) * u_ref[0, 2, f]
+        g[f] = (-7.0 / 24.0) * u_ref[0, f] + (1.0 / 3.0) * u_ref[1, f] - (1.0 / 24.0) * u_ref[2, f]
 
     @pl.when(p > 0)
     def _():
@@ -165,7 +174,7 @@
     for f in range(3):
         g[f] = (
             0.5 * s1[f]
-            - (1.0 / 24.0) * u_ref[0, 0, f] - (1.0 / 6.0) * u_ref[0, 1, f] + (5.0 / 24.0) * u_ref[0, 2, f]
+            - (1.0 / 24.0) * u_ref[0, f] - (1.0 / 6.0) * u_ref[1, f] + (5.0 / 24.0) * u_ref[2, f]
         )
     rates = rate_of_g(1)
     first = jnp.where(p == 0, 1.0, 0.0).astype(jnp.float32)
@@ -451,10 +460,11 @@
         vmem = pl.BlockSpec(memory_space=pltpu.VMEM)
         return pl.pallas_call(
             functools.partial(kernel, cfg),
-            out_shape=jax.ShapeDtypeStruct(fine_nodes.shape, f32),
-            in_specs=[vmem] * 3,
+            out_shape=pltpu.VMEM(fine_nodes.shape, f32),
+            in_specs=[pl.BlockSpec(memory_space=pl.ANY)] * 3,
             out_specs=vmem,
             scratch_shapes=[
+                pltpu.VMEM((3, 3, RL, NX), f32), state, pltpu.VMEM((RL, NX), f32),
                 state, state, state, state, state,
                 pltpu.VMEM((nh, RL, K * LANES), f32),
                 pltpu.VMEM((SP, RL, W + LANES), f32),
@@ -470,7 +480,7 @@
                 pltpu.VMEM((nh, R, LANES), f32),
                 dma, dma, dma((3, 2)), dma((3, 2)), dma((SP,)), dma, dma((2,)), dma((2, T // NG)),
                 dma, dma((GROUPS,)), dma((GROUPS,)), dma((GROUPS,)),
-                dma((2,)), dma((2,)), dma((members,)), dma,
+                dma((2,)), dma((2,)), dma((members,)), dma, dma((5,)),
             ],
             compiler_params=pltpu.CompilerParams(
                 collective_id=0, has_side_effects=True, vmem_limit_bytes=60 * 1024 * 1024

time: 68.5 us -> 64.2 us (0.937)
  Pallas kernels: 65.1 us -> 62.6 us
  local copies, waits for them, and re-layouts: 3.27 us -> 1.41 us
    pallas_call x1, Pallas kernels: 65.1 us -> 62.6 us  [per_device(): pl.pallas_call(functools.partial(kernel, cfg), out_shape=pltpu.VMEM(fine_...]
    unnamed x1, local copies, waits for them, and re-layouts: 3.27 us -> 1.41 us
where the time goes in v3:
time: 64.2 us; the launch traced here: 64.1 us
  Pallas kernels  62.6 us (98%)
  local copies, waits for them, and re-layouts  1.41 us (2%)
    pallas_call x1, Pallas kernels, per_device(): pl.pallas_call(functools.partial(kernel, cfg), out_shape=pltpu.VMEM(fine_...  62.6 us
    unnamed x1, local copies, waits for them, and re-layouts  1.41 us

profile of v3, /device:TPU:27, one launch (start us, length us, event | category | flops | bytes accessed | tf_op | source)
XLA Modules:
  0.0 64.1 jit_solution(2155460267462930013)
XLA Ops:
  0.0 62.6 %shard_map.37 = f32[1,3,3,16,4096]{4,3,2,1,0:T(8,128)S(1)} custom-call(f32[1,3,3,16,4096]{4,3,2,1,0:T(8,128)} %u_hbm.1, f32[3,16,4096]{2,1,0:T(8,128)} %init_hbm.1, f32[16,4096]{1,0:T(8,128)} %depth_hbm.1), custom_call_target="tpu_custom_call" | custom-call | tf_op jit(solution)/shard_map/pallas_call | solution.py:461
  62.6 1.4 %copy.5 = f32[1,3,3,16,4096]{4,3,2,1,0:T(8,128)} copy(f32[1,3,3,16,4096]{4,3,2,1,0:T(8,128)S(1)} %shard_map.37) | data formatting | bytes 4718592

commit v4 on v3

--- a/solution.py
+++ b/solution.py
@@ -186,6 +186,39 @@
     for f in range(3):
         b[f] = first * s0[f] + DT * rates[f]
 
+    my_rows = pl.ds(pl.multiple_of(y * RL, 8), RL)
+
+    def a2a(k):
+        ends = (
+            (b.at[:, :, pl.ds(pl.multiple_of(k * W, LANES), W)], main.at[pb, :, my_rows]),
+            (halo_src.at[:, :, pl.ds(pl.multiple_of(k * LANES, LANES), LANES)], halo.at[pb, :, my_rows]),
+        )
+        there = [
+            pltpu.make_async_remote_copy(
+                src_ref=src, dst_ref=dst, send_sem=a2a_s.at[i], recv_sem=a2a_r.at[i, pb],
+                device_id=where(block * TG * SP + k * stride), device_id_type=MESH,
+            )
+            for i, (src, dst) in enumerate(ends)
+        ]
+        here = [pltpu.make_async_copy(src, dst, a2a_r.at[i, pb]) for i, (src, dst) in enumerate(ends)]
+        return there, here
+
+    def spread(i):
+        @pl.loop(0, K)
+        def _(j):
+            k = lax.rem(mine + j, K)
+            there, here = a2a(k)
+
+            @pl.when(k * stride != local)
+            def _():
+                there[i].start()
+
+            @pl.when(k * stride == local)
+            def _():
+                here[i].start()
+
+    spread(0)
+
     slot_of = lax.rem(lane_h + hw, LANES) // (2 * hw)
     for k in range(K):
         lo, hi = ((k + 1) % K) * W, (k * W - LANES) % NX
@@ -199,37 +232,7 @@
         for i in range(nh):
             halo_src[i, :, k * LANES : (k + 1) * LANES] = packed[i]
 
-    my_rows = pl.ds(pl.multiple_of(y * RL, 8), RL)
-
-    def a2a(k):
-        ends = (
-            (b.at[:, :, pl.ds(pl.multiple_of(k * W, LANES), W)], main.at[pb, :, my_rows]),
-            (halo_src.at[:, :, pl.ds(pl.multiple_of(k * LANES, LANES), LANES)], halo.at[pb, :, my_rows]),
-        )
-        there = [
-            pltpu.make_async_remote_copy(
-                src_ref=src, dst_ref=dst, send_sem=a2a_s.at[i], recv_sem=a2a_r.at[i, pb],
-                device_id=where(block * TG * SP + k * stride), device_id_type=MESH,
-            )
-            for i, (src, dst) in enumerate(ends)
-        ]
-        here = [pltpu.make_async_copy(src, dst, a2a_r.at[i, pb]) for i, (src, dst) in enumerate(ends)]
-        return there, here
-
-    @pl.loop(0, K)
-    def _(i):
-        k = lax.rem(mine + i, K)
-        there, here = a2a(k)
-
-        @pl.when(k * stride != local)
-        def _():
-            for copy in there:
-                copy.start()
-
-        @pl.when(k * stride == local)
-        def _():
-            for copy in here:
-                copy.start()
+    spread(1)
 
     my_tile = pl.ds(pl.multiple_of(mine * W, LANES), W)
     my_group = mine // (K // GROUPS)

time: 64.2 us -> 65.5 us (1.020); the launches traced: 64.1 us -> 64.6 us
  no operation moved by 1% of the time
where the time goes in v4:
time: 65.5 us; the launch traced here: 64.6 us
  Pallas kernels  63.1 us (96%)
  local copies, waits for them, and re-layouts  1.41 us (2%)
    pallas_call x1, Pallas kernels, per_device(): pl.pallas_call(functools.partial(kernel, cfg), out_shape=pltpu.VMEM(fine_...  63.1 us
    unnamed x1, local copies, waits for them, and re-layouts  1.41 us

profile of v4, /device:TPU:27, one launch (start us, length us, event | category | flops | bytes accessed | tf_op | source)
XLA Modules:
  0.0 64.6 jit_solution(7252906475814251936)
XLA Ops:
  0.0 63.1 %shard_map.37 = f32[1,3,3,16,4096]{4,3,2,1,0:T(8,128)S(1)} custom-call(f32[1,3,3,16,4096]{4,3,2,1,0:T(8,128)} %u_hbm.1, f32[3,16,4096]{2,1,0:T(8,128)} %init_hbm.1, f32[16,4096]{1,0:T(8,128)} %depth_hbm.1), custom_call_target="tpu_custom_call" | custom-call | tf_op jit(solution)/shard_map/pallas_call | solution.py:464
  63.2 1.4 %copy.5 = f32[1,3,3,16,4096]{4,3,2,1,0:T(8,128)} copy(f32[1,3,3,16,4096]{4,3,2,1,0:T(8,128)S(1)} %shard_map.37) | data formatting | bytes 4718592
